TPU v7x, 32 devices: a whole 2x2x4 slice. The times are simulated.
32 devices in a mesh: tm: 16 (over z, x, core), mom: 2 (over y).
Axes of the slice: x: 2, y: 2, z: 4, core: 2. Of those that a mesh axis runs over, the one named last changes fastest.
Arguments:
- fields: bfloat16 [16, 4, 2, 512, 512], P('tm', 'mom'), may hold values from -1 to 1
- mom_pairs: int32 [6, 2], P('mom'), may hold values from 0 to 3, as said below
- deltas: int32 [4], replicated, may hold values from 0 to 3, each once
Outputs:
- time_traces: float32 [16, 2, 4, 6], P('tm', None, None, 'mom')
- summed_traces: float32 [2, 4, 6], P(None, None, 'mom')
Inputs may be any that keep to these rules, and one draw needn't show every extreme that they name: `mom_pairs`: column 0 may be any momentum; in row r, column 1 lies in momentum group r // 3, that is from (r // 3) * 2 to (r // 3) * 2 + 1.
All inputs are finite; a program needn't handle non-finite values.
Results may differ from a plain program's by a relative error of at most 0.0003.
Values may be sent and summed in bfloat16 or wider, within the bound.
A program may use at most 128 MiB of HBM per device.

v0:
```python
import functools

import jax
import jax.numpy as jnp
from jax import lax
from jax.experimental import pallas as pl
from jax.experimental.pallas import tpu as pltpu
from jax.sharding import PartitionSpec as P

MESH = pl.DeviceIdType.MESH
BLK = 128


def kernel(n_tm, n_mom, pair_ref, delta_ref, field_ref, local_ref, sum_ref, *scratch):
    per_group, _, nev, _ = field_ref.shape[1:]
    stages = nev // BLK
    slots = 4
    subs = per_group * 2
    pairs = pair_ref.shape[1]
    seps = delta_ref.shape[0]
    a_bufs = scratch[:stages]
    b_flat = scratch[stages : stages + stages * slots]
    b_bufs = [b_flat[n * slots : (n + 1) * slots] for n in range(stages)]
    acc_d, acc_b, held, gathered = scratch[stages + stages * slots : stages + stages * slots + 4]
    own_sem, y_send, y_recv, b_send, b_recv, r_send, r_recv = scratch[-7:]

    me = lax.axis_index("tm")
    group = lax.axis_index("mom")

    def at(step):
        return {"tm": lax.rem(me + step + n_tm, n_tm), "mom": group}

    upper_core = lax.rem(me, 2) == 1
    odd_chip = lax.rem(me // 2, 2) == 1

    own_copies = []
    for n in range(stages):
        copy = pltpu.make_async_copy(
            field_ref.at[0, :, :, pl.ds(n * BLK, BLK), :],
            a_bufs[n].at[pl.ds(group * per_group, per_group)],
            own_sem.at[n],
        )
        copy.start()
        own_copies.append(copy)

    barrier = pltpu.get_barrier_semaphore()

    def greet(i, carry):
        pl.semaphore_signal(barrier, inc=1, device_id=at(i), device_id_type=MESH)
        return carry

    lax.fori_loop(1, n_tm, greet, 0)
    for j in range(1, n_mom):
        pl.semaphore_signal(
            barrier, inc=1, device_id={"tm": me, "mom": lax.rem(group + j, n_mom)}, device_id_type=MESH
        )
    pl.semaphore_wait(barrier, n_tm - 1 + n_mom - 1)

    def own_part(n, sub):
        return field_ref.at[0, sub // 2, sub % 2, :, pl.ds(n * BLK, BLK)]

    def part(n, slot, sub):
        return b_bufs[n][slot - 1].at[sub // 2, sub % 2]

    def hop(src, n, slot, sub, step):
        return pltpu.make_async_remote_copy(
            src_ref=src,
            dst_ref=part(n, slot, sub),
            send_sem=b_send.at[slot - 1, n, sub],
            recv_sem=b_recv.at[slot - 1, n, sub],
            device_id=at(step),
            device_id_type=MESH,
        )

    def across(n, j):
        return pltpu.make_async_remote_copy(
            src_ref=field_ref.at[0, :, :, pl.ds(n * BLK, BLK), :],
            dst_ref=a_bufs[n].at[pl.ds(group * per_group, per_group)],
            send_sem=y_send.at[n, j],
            recv_sem=y_recv.at[n, j],
            device_id={"tm": me, "mom": lax.rem(group + j, n_mom)},
            device_id_type=MESH,
        )

    for n in range(stages):
        for j in range(1, n_mom):
            across(n, j).start()
        for sub in range(subs):
            hop(own_part(n, sub), n, 4, sub, -4).start()

        @pl.when(odd_chip)
        def _():
            for sub in range(subs):
                hop(own_part(n, sub), n, 2, sub, -2).start()

        @pl.when(upper_core)
        def _():
            for sub in range(subs):
                hop(own_part(n, sub), n, 1, sub, -1).start()

    def relay_four(n, sub):
        hop(part(n, 4, sub), n, 4, sub, -4).wait_recv()

        @pl.when(jnp.logical_not(odd_chip))
        def _():
            hop(part(n, 4, sub), n, 2, sub, 2).start()

        @pl.when(jnp.logical_not(upper_core))
        def _():
            hop(part(n, 4, sub), n, 3, sub, 1).start()

    def relay_two(n, sub):
        hop(part(n, 2, sub), n, 2, sub, -2).wait_recv()

        @pl.when(upper_core)
        def _():
            hop(part(n, 2, sub), n, 3, sub, -1).start()

        @pl.when(jnp.logical_not(upper_core))
        def _():
            hop(part(n, 2, sub), n, 1, sub, 1).start()

    acc_d[...] = jnp.zeros_like(acc_d)
    acc_b[...] = jnp.zeros_like(acc_b)
    eye = (
        lax.broadcasted_iota(jnp.int32, (BLK, BLK), 0) == lax.broadcasted_iota(jnp.int32, (BLK, BLK), 1)
    ).astype(jnp.float32)

    def fold(x):
        return jnp.sum(x.reshape(BLK // 8, 8, BLK), axis=0)

    def left(i, k):
        a = pair_ref[0, k]
        return jnp.concatenate([a_bufs[i][a, 0], a_bufs[i][a, 1]], axis=1)

    def right(i, slot, k):
        b = lax.rem(pair_ref[1, k], per_group)
        buf = b_bufs[i][slot - 1]
        re, im = buf[b, 0], buf[b, 1]
        return jnp.concatenate(
            [jnp.concatenate([re, im], axis=1), jnp.concatenate([-im, re], axis=1)], axis=0
        )

    def rows_of(n, slot):
        for k in range(pairs):
            lhs = left(n, k)
            for j in range(n):
                row = jnp.dot(lhs, right(j, slot, k), preferred_element_type=jnp.float32)
                index = (slot - 1) * pairs + k
                held[index, j, 0] = row[:, :BLK].T
                held[index, j, 1] = row[:, BLK:].T

    def columns_of(n, slot):
        for k in range(pairs):
            index = (slot - 1) * pairs + k
            column = jnp.dot(
                jnp.concatenate([left(i, k) for i in range(n + 1)], axis=0),
                right(n, slot, k),
                preferred_element_type=jnp.float32,
            )
            box = jnp.zeros((BLK, BLK), jnp.float32)
            for j in range(n):
                upper = column[j * BLK : (j + 1) * BLK]
                box += upper[:, :BLK] * held[index, j, 0] - upper[:, BLK:] * held[index, j, 1]
            corner = column[n * BLK :]
            re, im = corner[:, :BLK], corner[:, BLK:]
            box = box + box + re * re.T - im * im.T
            acc_b[index] += fold(box)
            acc_d[index] += fold(re * eye)

    order = (4, 2, 1, 3)
    share = [range(p * subs // slots, (p + 1) * subs // slots) for p in range(slots)]
    late = share[-1]
    for sub in range(subs):
        relay_four(0, sub)
        relay_two(0, sub)
    for n in range(stages):
        own_copies[n].wait()
        for j in range(1, n_mom):
            across(n, j).wait_recv()
        if n:
            for slot in order[: slots // 2]:
                rows_of(n, slot)
            for sub in late:
                relay_two(n, sub)
            for slot in order[slots // 2 :]:
                rows_of(n, slot)
        for place, slot in enumerate(order):
            if slot % 2 == 1:
                for sub in range(subs):
                    hop(part(n, slot, sub), n, slot, sub, -1).wait_recv()
            columns_of(n, slot)
            if n + 1 < stages:
                for sub in share[place]:
                    relay_four(n + 1, sub)
                    if place < slots - 1:
                        relay_two(n + 1, sub)

    count = acc_d.shape[0]
    height = gathered.shape[1]
    lane = lax.broadcasted_iota(jnp.int32, (1, BLK), 1)
    wanted = jnp.zeros((1, BLK), jnp.int32)
    for r in range(seps):
        wanted = jnp.where(lane == r, delta_ref[r], wanted)
    index = lax.broadcasted_iota(jnp.int32, (count, BLK), 0)
    which = lax.broadcasted_iota(jnp.int32, (height, BLK), 0)
    stat = jnp.zeros((height, BLK), jnp.float32)
    for p, acc in enumerate((acc_d, acc_b)):
        each = jnp.sum(jnp.sum(acc[...], axis=1), axis=1, keepdims=True)
        each = jnp.broadcast_to(each, (count, BLK))
        for k in range(pairs):
            line = jnp.sum(jnp.where(index == wanted * pairs + k, each, 0.0), axis=0, keepdims=True)
            stat = jnp.where(which == 2 * k + p, jnp.broadcast_to(line, (height, BLK)), stat)
    gathered[me] = stat

    def write(ref, value):
        for k in range(pairs):
            ref[k] = value[2 * k : 2 * k + 2, :seps]

    def give(i):
        return pltpu.make_async_remote_copy(
            src_ref=gathered.at[me],
            dst_ref=gathered.at[me],
            send_sem=r_send.at[i],
            recv_sem=r_recv.at[i],
            device_id=at(i),
            device_id_type=MESH,
        )

    far = sorted(range(1, n_tm), key=lambda i: -min(i, n_tm - i))
    for i in far:
        give(i).start()
    write(local_ref, stat)
    for n in range(stages):
        for j in range(1, n_mom):
            across(n, j).wait_send()
        for sub in range(subs):
            for slot in range(1, slots + 1):
                hop(part(n, slot, sub), n, slot, sub, -1).wait_send()

    for i in reversed(far):
        give(i).wait()
    write(sum_ref, jnp.sum(gathered[...], axis=0))


def per_device(n_tm, n_mom, fields, mom_pairs, deltas):
    _, per_group, _, nev, _ = fields.shape
    pairs = mom_pairs.shape[0]
    seps = deltas.shape[0]
    stages = nev // BLK
    subs = per_group * 2
    slots = 4
    rows = -(-seps * pairs // 8) * 8
    height = -(-2 * pairs // 8) * 8
    scratch = (
        [pltpu.VMEM((n_mom * per_group, 2, BLK, nev), fields.dtype)] * stages
        + [pltpu.VMEM((per_group, 2, nev, BLK), fields.dtype)] * (stages * slots)
        + [pltpu.VMEM((rows, 8, BLK), jnp.float32)] * 2
        + [pltpu.VMEM((rows, stages - 1, 2, BLK, BLK), jnp.float32)]
        + [pltpu.VMEM((n_tm, height, BLK), jnp.float32)]
        + [
            pltpu.SemaphoreType.DMA((stages,)),
            pltpu.SemaphoreType.DMA((stages, n_mom)),
            pltpu.SemaphoreType.DMA((stages, n_mom)),
            pltpu.SemaphoreType.DMA((slots, stages, subs)),
            pltpu.SemaphoreType.DMA((slots, stages, subs)),
            pltpu.SemaphoreType.DMA((n_tm,)),
            pltpu.SemaphoreType.DMA((n_tm,)),
        ]
    )
    tile = jax.ShapeDtypeStruct((pairs, 2, seps), jnp.float32)
    local, total = pl.pallas_call(
        functools.partial(kernel, n_tm, n_mom),
        out_shape=(tile, tile),
        in_specs=[
            pl.BlockSpec(memory_space=pltpu.SMEM),
            pl.BlockSpec(memory_space=pltpu.SMEM),
            pl.BlockSpec(memory_space=pltpu.HBM),
        ],
        out_specs=(pl.BlockSpec(memory_space=pltpu.VMEM), pl.BlockSpec(memory_space=pltpu.VMEM)),
        scratch_shapes=scratch,
        compiler_params=pltpu.CompilerParams(
            collective_id=0, has_side_effects=True, vmem_limit_bytes=67_043_328
        ),
    )(mom_pairs.T, deltas, fields)

    return (local.transpose(1, 2, 0)[None], total.transpose(1, 2, 0))


def solution(mesh):
    return jax.shard_map(
        functools.partial(per_device, mesh.shape["tm"], mesh.shape["mom"]),
        mesh=mesh,
        in_specs=(P("tm", "mom", None, None, None), P("mom", None), P()),
        out_specs=(P("tm", None, None, "mom"), P(None, None, "mom")),
        check_vma=False,
    )
```

profile of v0, /device:TPU:0, one launch (start us, length us, event | category | flops | bytes accessed | tf_op | source)
XLA Modules:
  0.0 75.7 jit_solution(915643534377868664)
XLA Ops:
  0.6 72.6 %shard_map.50 = (f32[3,2,4]{2,1,0:T(2,128)}, f32[3,2,4]{2,1,0:T(2,128)}) custom-call(s32[2,3]{1,0:T(2,128)} %bitcast.7, s32[4]{0:T(128)} %delta_ref.1, bf16[1,2,2,512,512]{4,3,2,1,0:T(8,128)(2,1)} %field_ref.1), custom_call_target="tpu_custom_call" | custom-call | tf_op jit(solution)/shard_map/pallas_call | solution.py:272
  73.2 1.3 %copy.7 = f32[1,2,4,3]{2,1,3,0:T(2,128)} copy(f32[1,2,4,3]{2,1,3,0:T(2,128)} %bitcast.6) | data formatting | bytes 192
  74.4 1.2 %copy.8 = f32[2,4,3]{1,0,2:T(2,128)} copy(f32[2,4,3]{1,0,2:T(2,128)} %bitcast.5) | data formatting | bytes 192
where the time goes:
time: 75.9 us; the launch traced here: 75.7 us
  Pallas kernels  72.6 us (96%)
  local copies, waits for them, and re-layouts  2.49 us (3%)
    pallas_call x1, Pallas kernels, per_device(): pl.pallas_call(functools.partial(kernel, n_tm, n_mom), out_shape=(tile, t...  72.6 us
    unnamed x2, local copies, waits for them, and re-layouts  2.49 us

commit v1 on v0

v1 whole, which is shorter than its diff:
```python
import functools

import jax
import jax.numpy as jnp
from jax import lax
from jax.experimental import pallas as pl
from jax.experimental.pallas import tpu as pltpu
from jax.sharding import PartitionSpec as P

MESH = pl.DeviceIdType.MESH
BLK = 128
ROWS = 64
LAG = 3
EARLY = 1


def kernel(n_tm, n_mom, pair_ref, delta_ref, field_ref, out_ref, *scratch):
    per_group, _, nev, _ = field_ref.shape[1:]
    stages = nev // BLK
    slots = 4
    pairs = pair_ref.shape[1]
    seps = delta_ref.shape[0]
    halves = BLK // ROWS
    parts = per_group * 2
    groups = stages * halves
    steps = groups * parts
    columns = n_tm // 4
    a_bufs = scratch[:stages]
    banks = [scratch[stages + q * groups : stages + (q + 1) * groups] for q in range(slots + 1)]
    b_bufs, own = banks[:slots], banks[slots]
    early, acc_d, acc_b, held, gathered = scratch[stages + (slots + 1) * groups :][:5]
    (own_sem, left_sem, y_send, y_recv, far_send, far_recv, b_send, b_recv, e_send, e_recv, f_send, r_send, r_recv,
     chain, rounds) = scratch[-15:]

    me = lax.axis_index("tm")
    group = lax.axis_index("mom")
    core = lax.rem(me, 2)
    upper_core = core == 1
    lower_core = core == 0
    odd_chip = lax.rem(me // 2, 2) == 1
    even_chip = lax.rem(me // 2, 2) == 0
    level = me // 4
    first_level = level == 0
    last_level = level == columns - 1

    def at(step):
        return {"tm": lax.rem(me + step + n_tm, n_tm), "mom": group}

    beside = {"tm": me + 2 - 4 * lax.rem(me // 2, 2), "mom": group}
    twin = {"tm": me + 1 - 2 * core, "mom": group}
    below = at(-4)
    above = at(4)
    across_from = [{"tm": me, "mom": lax.rem(group + j, n_mom)} for j in range(1, n_mom)]

    barrier = pltpu.get_barrier_semaphore()

    def greet(device):
        pl.semaphore_signal(barrier, inc=1, device_id=device, device_id_type=MESH)

    @pl.when(jnp.logical_not(first_level))
    def _():
        greet(below)

    @pl.when(jnp.logical_not(last_level))
    def _():
        greet(above)

    for device in [beside, twin] + across_from:
        greet(device)

    def load_own(g):
        return pltpu.make_async_copy(field_ref.at[0, :, :, pl.ds(g * ROWS, ROWS), :], own[g], own_sem.at[g])

    def load_left(n):
        return pltpu.make_async_copy(
            field_ref.at[0, :, :, :, pl.ds(n * BLK, BLK)],
            a_bufs[n].at[pl.ds(group * per_group, per_group)],
            left_sem.at[n],
        )

    for g in range(groups):
        load_own(g).start()
    for n in range(stages):
        load_left(n).start()
    for g in range(groups):
        load_own(g).wait()

    ends = jnp.where(first_level, 1, 0) + jnp.where(last_level, 1, 0)
    pl.semaphore_wait(barrier, n_mom + 3 - ends)

    def pass_chain():
        pl.semaphore_signal(chain, inc=1, device_id=below, device_id_type=MESH)

    if columns > 2:
        pl.when(level == columns - 2)(pass_chain)

    def piece(buf, i):
        g, rest = divmod(i, parts)
        return buf[g].at[rest // 2, rest % 2]

    def far(i, src):
        return pltpu.make_async_remote_copy(
            src_ref=piece(src, i),
            dst_ref=piece(b_bufs[0], i),
            send_sem=far_send.at[i],
            recv_sem=far_recv.at[i],
            device_id=below,
            device_id_type=MESH,
        )

    def near(q, g, src):
        return pltpu.make_async_remote_copy(
            src_ref=src[g],
            dst_ref=b_bufs[q][g],
            send_sem=b_send.at[q - 1, g],
            recv_sem=b_recv.at[q - 1, g],
            device_id=beside if q == 1 else twin,
            device_id_type=MESH,
        )

    def near_piece(i, src):
        return pltpu.make_async_remote_copy(
            src_ref=piece(src, i),
            dst_ref=piece(b_bufs[1], i),
            send_sem=b_send.at[0, i // parts],
            recv_sem=b_recv.at[0, i // parts],
            device_id=beside,
            device_id_type=MESH,
        )

    detour = range(steps - EARLY, steps)

    def give_early(i):
        return pltpu.make_async_remote_copy(
            src_ref=piece(own, i),
            dst_ref=early.at[i - detour[0]],
            send_sem=e_send.at[i - detour[0]],
            recv_sem=e_recv.at[i - detour[0]],
            device_id=beside,
            device_id_type=MESH,
        )

    def pass_early(i):
        return pltpu.make_async_remote_copy(
            src_ref=early.at[i - detour[0]],
            dst_ref=piece(b_bufs[1], i),
            send_sem=f_send.at[i - detour[0]],
            recv_sem=b_recv.at[0, i // parts],
            device_id=below,
            device_id_type=MESH,
        )

    def across(n, j):
        part = a_bufs[n].at[pl.ds(group * per_group, per_group)]
        return pltpu.make_async_remote_copy(
            src_ref=part,
            dst_ref=part,
            send_sem=y_send.at[n, j],
            recv_sem=y_recv.at[n, j],
            device_id=across_from[j],
            device_id_type=MESH,
        )

    def send_far(some):
        for i in some:
            far(i, own).start()

    if EARLY:

        @pl.when(even_chip)
        def _():
            for i in detour:
                give_early(i).start()

    for n in range(stages):
        @pl.when(jnp.logical_not(first_level))
        def _():
            send_far(range(n * halves * parts, (n + 1) * halves * parts))

        load_left(n).wait()
        for j in range(n_mom - 1):
            across(n, j).start()

        @pl.when(odd_chip)
        def _():
            for g in range(n * halves, (n + 1) * halves):
                near(1, g, own).start()

        @pl.when(upper_core)
        def _():
            for g in range(n * halves, (n + 1) * halves):
                near(2, g, own).start()

    if columns > 2:

        @pl.when(jnp.logical_and(level < columns - 2, jnp.logical_not(first_level)))
        def _():
            pl.semaphore_wait(chain, 1)
            pass_chain()

        @pl.when(first_level)
        def _():
            pl.semaphore_wait(chain, 1)

    @pl.when(first_level)
    def _():
        send_far(range(steps))

    if EARLY:

        @pl.when(odd_chip)
        def _():
            for i in detour:
                give_early(i).wait_recv()
                pass_early(i).start()

    def pass_far(i):
        far(i, b_bufs[0]).wait_recv()
        if i not in detour:

            @pl.when(even_chip)
            def _():
                near_piece(i, b_bufs[0]).start()

        if i % parts == parts - 1:

            @pl.when(lower_core)
            def _():
                near(2, i // parts, b_bufs[0]).start()

    def pass_near(g):
        near(1, g, b_bufs[1]).wait_recv()
        near(3, g, b_bufs[1]).start()

    def meet(r, devices):
        for device in devices:
            pl.semaphore_signal(rounds.at[r], inc=1, device_id=device, device_id_type=MESH)
        pl.semaphore_wait(rounds.at[r], len(devices))

    reach = 4
    meetings = []
    while 2 * reach < n_tm:
        meetings.append([at(-reach), at(reach)])
        reach *= 2
    meetings += [[beside], [twin]]

    acc_d[...] = jnp.zeros_like(acc_d)
    acc_b[...] = jnp.zeros_like(acc_b)
    eye = (
        lax.broadcasted_iota(jnp.int32, (BLK, BLK), 0) == lax.broadcasted_iota(jnp.int32, (BLK, BLK), 1)
    ).astype(jnp.float32)

    def fold(x):
        return jnp.sum(x.reshape(x.shape[0] // 8, 8, BLK), axis=0)

    def weight(n, k):
        a = pair_ref[0, k]
        re, im = a_bufs[n][a, 0], a_bufs[n][a, 1]
        return jnp.concatenate(
            [jnp.concatenate([re, im], axis=1), jnp.concatenate([-im, re], axis=1)], axis=0
        )

    def rows(q, some, k):
        b = lax.rem(pair_ref[1, k], per_group)
        return jnp.concatenate(
            [jnp.concatenate([b_bufs[q][g][b, 0], b_bufs[q][g][b, 1]], axis=1) for g in some], axis=0
        )

    def columns_of(n, k):
        product = jnp.dot(
            jnp.concatenate([rows(q, range(n * halves), k) for q in range(slots)], axis=0),
            weight(n, k),
            preferred_element_type=jnp.float32,
        )
        for q in range(slots):
            for m in range(n):
                block = product[(q * n + m) * BLK : (q * n + m + 1) * BLK]
                held[q * pairs + k, m, 0] = block[:, :BLK].T
                held[q * pairs + k, m, 1] = block[:, BLK:].T

    def rows_of(n, qs, k, part=None):
        some = range(halves) if part is None else [part]
        begin, size = some[0] * ROWS, len(some) * ROWS
        lhs = jnp.concatenate([rows(q, [n * halves + h for h in some], k) for q in qs], axis=0)
        span = pl.ds(begin, size)
        box = [None] * len(qs)
        for m in range(n, -1, -1):
            product = jnp.dot(lhs, weight(m, k), preferred_element_type=jnp.float32)
            for p, q in enumerate(qs):
                index = q * pairs + k
                re, im = product[p * size : (p + 1) * size, :BLK], product[p * size : (p + 1) * size, BLK:]
                if m < n:
                    box[p] += fold(re * held[index, m, 0, span] - im * held[index, m, 1, span])
                    continue
                box[p] = jnp.zeros((8, BLK), jnp.float32)
                if begin + size < BLK:
                    held[index, n, 0, span] = re
                    held[index, n, 1, span] = im
                    continue
                if begin:
                    re = jnp.concatenate([held[index, n, 0, pl.ds(0, begin)], re], axis=0)
                    im = jnp.concatenate([held[index, n, 1, pl.ds(0, begin)], im], axis=0)
                acc_d[index] += fold(re * eye)
                acc_b[index] += fold(re * re.T - im * im.T)
        if n:
            for p, q in enumerate(qs):
                acc_b[q * pairs + k] += box[p] + box[p]

    def lefts(n):
        for j in range(n_mom - 1):
            across(n, j).wait_recv()

    def work(n, j):
        if j == 0:
            lefts(n)
        if n:
            for k in range(pairs)[j::3] if j < 3 else ():
                columns_of(n, k)
        if j == 3:
            for g in range(n * halves, (n + 1) * halves):
                near(2, g, b_bufs[2]).wait_recv()
            rows_of(n, (0, 2), 0)
        if j == 4:
            for k in range(1, pairs):
                rows_of(n, (0, 2), k)
        if j == 5:
            for g in range(n * halves, (n + 1) * halves):
                near(3, g, b_bufs[3]).wait_recv()
            rows_of(n, (1, 3), 0)
        if j == 6:
            for k in range(1, pairs):
                rows_of(n, (1, 3), k)

    per_stage = halves * parts
    for i in range(steps):
        pass_far(i)
        g, rest = divmod(i - LAG, parts)
        if g >= 0 and rest == parts - 1:
            pass_near(g)
        if i % 4 == 1 and i // 4 < len(meetings):
            meet(i // 4, meetings[i // 4])
        if i >= per_stage:
            work(i // per_stage - 1, i % per_stage)
    last = stages - 1
    lefts(last)
    for k in range(pairs):
        columns_of(last, k)
    for h in range(halves):
        g = last * halves + h
        near(2, g, b_bufs[2]).wait_recv()
        if h == halves - 1:
            pass_near(g)
        for k in range(pairs):
            rows_of(last, (0, 2), k, h)
        near(3, g, b_bufs[3]).wait_recv()
        for k in range(pairs):
            rows_of(last, (1, 3), k, h)

    count = acc_d.shape[0]
    height = gathered.shape[1]
    lane = lax.broadcasted_iota(jnp.int32, (1, BLK), 1)
    wanted = jnp.zeros((1, BLK), jnp.int32)
    for r in range(seps):
        wanted = jnp.where(lane == r, delta_ref[r], wanted)
    place = jnp.where(wanted == 0, 2 + core, jnp.where(wanted == 1, 1, jnp.where(wanted == 2, 3 - core, 0)))
    index = lax.broadcasted_iota(jnp.int32, (count, BLK), 0)
    which = lax.broadcasted_iota(jnp.int32, (height, BLK), 0)
    stat = jnp.zeros((height, BLK), jnp.float32)
    for p, acc in enumerate((acc_d, acc_b)):
        each = jnp.sum(jnp.sum(acc[...], axis=1), axis=1, keepdims=True)
        each = jnp.broadcast_to(each, (count, BLK))
        for k in range(pairs):
            line = jnp.sum(jnp.where(index == place * pairs + k, each, 0.0), axis=0, keepdims=True)
            stat = jnp.where(which == 2 * k + p, jnp.broadcast_to(line, (height, BLK)), stat)
    gathered[me] = stat

    def give(i):
        return pltpu.make_async_remote_copy(
            src_ref=gathered.at[me],
            dst_ref=gathered.at[me],
            send_sem=r_send.at[i],
            recv_sem=r_recv.at[i],
            device_id=at(i),
            device_id_type=MESH,
        )

    order = sorted(range(1, n_tm), key=lambda i: -min(i, n_tm - i))
    for i in order:
        give(i).start()
    out_ref[0] = stat
    for n in range(stages):
        for j in range(n_mom - 1):
            across(n, j).wait_send()
    for i in range(steps):
        far(i, own).wait_send()
    for g in range(groups):
        for q in range(2, slots):
            near(q, g, own).wait_send()

    @pl.when(odd_chip)
    def _():
        for g in range(groups):
            near(1, g, own).wait_send()
        for i in detour:
            pass_early(i).wait_send()

    @pl.when(even_chip)
    def _():
        for g in range(groups):
            kept = [i for i in range(g * parts, (g + 1) * parts) if i not in detour]
            if len(kept) == parts:
                near(1, g, own).wait_send()
            else:
                for i in kept:
                    near_piece(i, own).wait_send()
        for i in detour:
            give_early(i).wait_send()

    for i in reversed(order):
        give(i).wait()
    out_ref[1] = jnp.sum(gathered[...], axis=0)


def split(stat_ref, local_ref, sum_ref):
    pairs, _, seps = local_ref.shape
    for ref, place in ((local_ref, 0), (sum_ref, 1)):
        for k in range(pairs):
            ref[k] = stat_ref[place, 2 * k : 2 * k + 2, :seps]


def per_device(n_tm, n_mom, fields, mom_pairs, deltas):
    _, per_group, _, nev, _ = fields.shape
    pairs = mom_pairs.shape[0]
    seps = deltas.shape[0]
    stages = nev // BLK
    slots = 4
    groups = nev // ROWS
    steps = groups * per_group * 2
    meetings = 2
    reach = 4
    while 2 * reach < n_tm:
        meetings += 1
        reach *= 2
    count = -(-slots * pairs // 8) * 8
    height = -(-2 * pairs // 8) * 8
    dma = pltpu.SemaphoreType.DMA
    scratch = (
        [pltpu.VMEM((n_mom * per_group, 2, nev, BLK), fields.dtype)] * stages
        + [pltpu.VMEM((per_group, 2, ROWS, nev), fields.dtype)] * (groups * (slots + 1))
        + [pltpu.VMEM((max(EARLY, 1), ROWS, nev), fields.dtype)]
        + [pltpu.VMEM((count, 8, BLK), jnp.float32)] * 2
        + [pltpu.VMEM((count, stages, 2, BLK, BLK), jnp.float32)]
        + [pltpu.VMEM((n_tm, height, BLK), jnp.float32)]
        + [dma((groups,)), dma((stages,))]
        + [dma((stages, n_mom))] * 2
        + [dma((steps,))] * 2
        + [dma((slots - 1, groups))] * 2
        + [dma((max(EARLY, 1),))] * 3
        + [dma((n_tm,))] * 2
        + [pltpu.SemaphoreType.REGULAR, pltpu.SemaphoreType.REGULAR((meetings,))]
    )
    stat = pl.pallas_call(
        functools.partial(kernel, n_tm, n_mom),
        out_shape=jax.ShapeDtypeStruct((2, height, BLK), jnp.float32),
        in_specs=[
            pl.BlockSpec(memory_space=pltpu.SMEM),
            pl.BlockSpec(memory_space=pltpu.SMEM),
            pl.BlockSpec(memory_space=pltpu.HBM),
        ],
        out_specs=pl.BlockSpec(memory_space=pltpu.VMEM),
        scratch_shapes=scratch,
        compiler_params=pltpu.CompilerParams(
            collective_id=0, has_side_effects=True, vmem_limit_bytes=67_043_328
        ),
    )(mom_pairs.T, deltas, fields)
    tile = jax.ShapeDtypeStruct((pairs, 2, seps), jnp.float32)
    local, total = pl.pallas_call(
        split,
        out_shape=(tile, tile),
        in_specs=[pl.BlockSpec(memory_space=pltpu.VMEM)],
        out_specs=(pl.BlockSpec(memory_space=pltpu.VMEM), pl.BlockSpec(memory_space=pltpu.VMEM)),
    )(stat)
    return (local.transpose(1, 2, 0)[None], total.transpose(1, 2, 0))


def solution(mesh):
    return jax.shard_map(
        functools.partial(per_device, mesh.shape["tm"], mesh.shape["mom"]),
        mesh=mesh,
        in_specs=(P("tm", "mom", None, None, None), P("mom", None), P()),
        out_specs=(P("tm", None, None, "mom"), P(None, None, "mom")),
        check_vma=False,
    )
```

time: 75.9 us -> 73.7 us (0.971)
  local copies, waits for them, and re-layouts: 2.49 us -> 0 us
    unnamed x2 -> x0, local copies, waits for them, and re-layouts: 2.49 us -> none
    pallas_call x1 -> x2, Pallas kernels: 72.6 us -> 72.8 us  [the longest x1 71.5 us: per_device(): pl.pallas_call(functools.partial(kernel, n_tm, n_mom), out_shape=jax.Shap...]
where the time goes in v1:
time: 73.7 us; the launch traced here: 73.4 us
  Pallas kernels  72.8 us (99%)
    pallas_call x1, Pallas kernels, per_device(): pl.pallas_call(functools.partial(kernel, n_tm, n_mom), out_shape=jax.Shap...  71.5 us

profile of v1, /device:TPU:0, one launch (start us, length us, event | category | flops | bytes accessed | tf_op | source)
XLA Modules:
  0.0 73.4 jit_solution(16988694765984376163)
XLA Ops:
  0.6 71.5 %shard_map.50.stat_ref = f32[2,8,128]{2,1,0:T(8,128)} custom-call(s32[2,3]{1,0:T(2,128)} %bitcast.5, s32[4]{0:T(128)} %delta_ref.1, bf16[1,2,2,512,512]{4,3,2,1,0:T(8,128)(2,1)} %field_ref.1), custom_call_target="tpu_custom_call" | custom-call | tf_op jit(solution)/shard_map/pallas_call | solution.py:462
  72.1 1.3 %shard_map.51 = (f32[3,2,4]{2,1,0:T(2,128)}, f32[3,2,4]{2,1,0:T(2,128)}) custom-call(f32[2,8,128]{2,1,0:T(8,128)} %shard_map.50.stat_ref), custom_call_target="tpu_custom_call" | custom-call | tf_op jit(solution)/shard_map/pallas_call | solution.py:477

commit v2 on v1

--- a/solution.py
+++ b/solution.py
@@ -28,7 +28,7 @@
     a_bufs = scratch[:stages]
     banks = [scratch[stages + q * groups : stages + (q + 1) * groups] for q in range(slots + 1)]
     b_bufs, own = banks[:slots], banks[slots]
-    early, acc_d, acc_b, held, gathered = scratch[stages + (slots + 1) * groups :][:5]
+    early, acc_d, acc_b, held, kept_rows, gathered = scratch[stages + (slots + 1) * groups :][:6]
     (own_sem, left_sem, y_send, y_recv, far_send, far_recv, b_send, b_recv, e_send, e_recv, f_send, r_send, r_recv,
      chain, rounds) = scratch[-15:]
 
@@ -78,12 +78,10 @@
             left_sem.at[n],
         )
 
-    for g in range(groups):
-        load_own(g).start()
     for n in range(stages):
+        for g in range(n * halves, (n + 1) * halves):
+            load_own(g).start()
         load_left(n).start()
-    for g in range(groups):
-        load_own(g).wait()
 
     ends = jnp.where(first_level, 1, 0) + jnp.where(last_level, 1, 0)
     pl.semaphore_wait(barrier, n_mom + 3 - ends)
@@ -167,12 +165,19 @@
 
     if EARLY:
 
+        for g in range(detour[0] // parts, groups):
+            load_own(g).wait()
+
         @pl.when(even_chip)
         def _():
             for i in detour:
                 give_early(i).start()
 
     for n in range(stages):
+        for g in range(n * halves, (n + 1) * halves):
+            if g * parts + parts <= detour[0]:
+                load_own(g).wait()
+
         @pl.when(jnp.logical_not(first_level))
         def _():
             send_far(range(n * halves * parts, (n + 1) * halves * parts))
@@ -232,10 +237,11 @@
         near(1, g, b_bufs[1]).wait_recv()
         near(3, g, b_bufs[1]).start()
 
-    def meet(r, devices):
-        for device in devices:
+    def meet(r):
+        if r:
+            pl.semaphore_wait(rounds.at[r - 1], len(meetings[r - 1]))
+        for device in meetings[r] if r < len(meetings) else ():
             pl.semaphore_signal(rounds.at[r], inc=1, device_id=device, device_id_type=MESH)
-        pl.semaphore_wait(rounds.at[r], len(devices))
 
     reach = 4
     meetings = []
@@ -266,7 +272,7 @@
             [jnp.concatenate([b_bufs[q][g][b, 0], b_bufs[q][g][b, 1]], axis=1) for g in some], axis=0
         )
 
-    def columns_of(n, k):
+    def columns_of(n, k, kept=()):
         product = jnp.dot(
             jnp.concatenate([rows(q, range(n * halves), k) for q in range(slots)], axis=0),
             weight(n, k),
@@ -275,16 +281,29 @@
         for q in range(slots):
             for m in range(n):
                 block = product[(q * n + m) * BLK : (q * n + m + 1) * BLK]
-                held[q * pairs + k, m, 0] = block[:, :BLK].T
-                held[q * pairs + k, m, 1] = block[:, BLK:].T
-
-    def rows_of(n, qs, k, part=None):
+                index = q * pairs + k
+                re, im = block[:, :BLK].T, block[:, BLK:].T
+                held[index, m, 0] = re
+                held[index, m, 1] = im
+                if q in kept:
+                    box = fold(kept_rows[index, m, 0] * re[:ROWS] - kept_rows[index, m, 1] * im[:ROWS])
+                    acc_b[index] += box + box
+
+    def keep_rows(n, qs, k):
+        lhs = jnp.concatenate([rows(q, [n * halves], k) for q in qs], axis=0)
+        for m in range(n):
+            product = jnp.dot(lhs, weight(m, k), preferred_element_type=jnp.float32)
+            for p, q in enumerate(qs):
+                kept_rows[q * pairs + k, m, 0] = product[p * ROWS : (p + 1) * ROWS, :BLK]
+                kept_rows[q * pairs + k, m, 1] = product[p * ROWS : (p + 1) * ROWS, BLK:]
+
+    def rows_of(n, qs, k, part=None, lowest=0):
         some = range(halves) if part is None else [part]
         begin, size = some[0] * ROWS, len(some) * ROWS
         lhs = jnp.concatenate([rows(q, [n * halves + h for h in some], k) for q in qs], axis=0)
         span = pl.ds(begin, size)
         box = [None] * len(qs)
-        for m in range(n, -1, -1):
+        for m in range(n, lowest - 1, -1):
             product = jnp.dot(lhs, weight(m, k), preferred_element_type=jnp.float32)
             for p, q in enumerate(qs):
                 index = q * pairs + k
@@ -302,7 +321,7 @@
                     im = jnp.concatenate([held[index, n, 1, pl.ds(0, begin)], im], axis=0)
                 acc_d[index] += fold(re * eye)
                 acc_b[index] += fold(re * re.T - im * im.T)
-        if n:
+        if lowest < n:
             for p, q in enumerate(qs):
                 acc_b[q * pairs + k] += box[p] + box[p]
 
@@ -310,51 +329,110 @@
         for j in range(n_mom - 1):
             across(n, j).wait_recv()
 
-    def work(n, j):
-        if j == 0:
-            lefts(n)
+    def columns_all(n, ks=None, kept=()):
         if n:
-            for k in range(pairs)[j::3] if j < 3 else ():
-                columns_of(n, k)
-        if j == 3:
-            for g in range(n * halves, (n + 1) * halves):
-                near(2, g, b_bufs[2]).wait_recv()
-            rows_of(n, (0, 2), 0)
-        if j == 4:
-            for k in range(1, pairs):
-                rows_of(n, (0, 2), k)
-        if j == 5:
-            for g in range(n * halves, (n + 1) * halves):
-                near(3, g, b_bufs[3]).wait_recv()
-            rows_of(n, (1, 3), 0)
-        if j == 6:
-            for k in range(1, pairs):
-                rows_of(n, (1, 3), k)
-
-    per_stage = halves * parts
-    for i in range(steps):
+            for k in range(pairs) if ks is None else ks:
+                columns_of(n, k, kept)
+
+    def rows_all(n, qs, part=None, ks=None):
+        for k in range(pairs) if ks is None else ks:
+            rows_of(n, qs, k, part)
+
+    def twins(q, some):
+        for g in some:
+            near(q, g, b_bufs[q]).wait_recv()
+
+    def of(n):
+        return range(n * halves, (n + 1) * halves)
+
+    def step(i):
         pass_far(i)
         g, rest = divmod(i - LAG, parts)
         if g >= 0 and rest == parts - 1:
             pass_near(g)
-        if i % 4 == 1 and i // 4 < len(meetings):
-            meet(i // 4, meetings[i // 4])
+        r, rest = divmod(i - 1, pace)
+        if i and rest == 0 and r <= len(meetings):
+            meet(r)
+
+    def plain(n):
+        first, second = range(0, (pairs + 1) // 2), range((pairs + 1) // 2, pairs)
+        return [
+            lambda: (lefts(n), columns_all(n, [0])),
+            lambda: columns_all(n, first[1:]),
+            lambda: columns_all(n, second),
+            lambda: (twins(2, of(n)), rows_all(n, (0, 2), None, [0])),
+            lambda: rows_all(n, (0, 2), None, range(1, pairs)),
+            lambda: (twins(3, of(n)), rows_all(n, (1, 3), None, [0])),
+            lambda: rows_all(n, (1, 3), None, range(1, pairs)),
+        ]
+
+    per_stage = halves * parts
+    last = stages - 1
+    pace = min(6, (steps - 2) // len(meetings))
+    for i in range(per_stage * last):
+        step(i)
         if i >= per_stage:
-            work(i // per_stage - 1, i % per_stage)
-    last = stages - 1
-    lefts(last)
-    for k in range(pairs):
-        columns_of(last, k)
-    for h in range(halves):
-        g = last * halves + h
-        near(2, g, b_bufs[2]).wait_recv()
-        if h == halves - 1:
-            pass_near(g)
+            units = plain(i // per_stage - 1)
+            if i % per_stage < len(units):
+                units[i % per_stage]()
+
+    @pl.when(jnp.logical_not(last_level))
+    def _():
+        n = last - 1
+        units = [
+            lambda: (lefts(n), columns_all(n, [0])),
+            lambda: columns_all(n, range(1, pairs)),
+            lambda: (twins(2, of(n)), rows_all(n, (0, 2), None, range(pairs - 1))),
+            lambda: (rows_all(n, (0, 2), None, [pairs - 1]), twins(3, of(n)), rows_all(n, (1, 3), None, [0])),
+            lambda: rows_all(n, (1, 3), None, range(1, pairs)),
+            lambda: (twins(2, of(last)[:1]), [keep_rows(last, (0, 2), k) for k in range(pairs)]),
+        ]
+        for j in range(per_stage):
+            step(per_stage * last + j)
+            if j < len(units):
+                units[j]()
+        twins(3, of(last)[:1])
         for k in range(pairs):
-            rows_of(last, (0, 2), k, h)
-        near(3, g, b_bufs[3]).wait_recv()
+            keep_rows(last, (1, 3), k)
+        lefts(last)
+        columns_all(last, kept=range(slots))
         for k in range(pairs):
-            rows_of(last, (1, 3), k, h)
+            rows_of(last, range(slots), k, 0, last)
+        g = groups - 1
+        twins(2, [g])
+        pass_near(g)
+        rows_all(last, (0, 2), halves - 1)
+        twins(3, [g])
+        rows_all(last, (1, 3), halves - 1)
+
+    @pl.when(last_level)
+    def _():
+        begin = per_stage * last
+        n = last - 1
+        units = [
+            lambda: (lefts(n), columns_all(n)),
+            lambda: (twins(2, of(n)), rows_all(n, (0, 2), None, range(pairs - 1))),
+            lambda: rows_all(n, (0, 2), None, range(pairs - 1, pairs)),
+            lambda: (twins(3, of(n)), rows_all(n, (1, 3))),
+            lambda: (twins(2, of(last)[:1]), [keep_rows(last, (0, 2), k) for k in range(pairs)]),
+            lambda: (lefts(last), columns_all(last, [0], (0, 2))),
+            lambda: (
+                columns_all(last, range(1, pairs), (0, 2)),
+                [rows_of(last, (0, 2), k, 0, last) for k in range(pairs)],
+                twins(3, of(last)[:1]),
+                rows_all(last, (1, 3), 0),
+            ),
+        ]
+        for j in range(per_stage):
+            step(begin + j)
+            if j < len(units):
+                units[j]()
+        g = groups - 1
+        twins(2, [g])
+        pass_near(g)
+        rows_all(last, (0, 2), halves - 1)
+        twins(3, [g])
+        rows_all(last, (1, 3), halves - 1)
 
     count = acc_d.shape[0]
     height = gathered.shape[1]
@@ -450,6 +528,7 @@
         + [pltpu.VMEM((max(EARLY, 1), ROWS, nev), fields.dtype)]
         + [pltpu.VMEM((count, 8, BLK), jnp.float32)] * 2
         + [pltpu.VMEM((count, stages, 2, BLK, BLK), jnp.float32)]
+        + [pltpu.VMEM((count, stages - 1, 2, ROWS, BLK), jnp.float32)]
         + [pltpu.VMEM((n_tm, height, BLK), jnp.float32)]
         + [dma((groups,)), dma((stages,))]
         + [dma((stages, n_mom))] * 2

time: 73.7 us -> 71.8 us (0.974)
  Pallas kernels: 72.8 us -> 70.9 us
    pallas_call x1, Pallas kernels: 71.5 us -> 69.6 us  [per_device(): pl.pallas_call(functools.partial(kernel, n_tm, n_mom), out_shape=jax.Shap...]
where the time goes in v2:
time: 71.8 us; the launch traced here: 71.5 us
  Pallas kernels  70.9 us (99%)
    pallas_call x1, Pallas kernels, per_device(): pl.pallas_call(functools.partial(kernel, n_tm, n_mom), out_shape=jax.Shap...  69.6 us

profile of v2, /device:TPU:0, one launch (start us, length us, event | category | flops | bytes accessed | tf_op | source)
XLA Modules:
  0.0 71.5 jit_solution(10441424776774262579)
XLA Ops:
  0.6 69.6 %shard_map.50.stat_ref = f32[2,8,128]{2,1,0:T(8,128)} custom-call(s32[2,3]{1,0:T(2,128)} %bitcast.5, s32[4]{0:T(128)} %delta_ref.1, bf16[1,2,2,512,512]{4,3,2,1,0:T(8,128)(2,1)} %field_ref.1), custom_call_target="tpu_custom_call" | custom-call | tf_op jit(solution)/shard_map/pallas_call | solution.py:541
  70.3 1.3 %shard_map.51 = (f32[3,2,4]{2,1,0:T(2,128)}, f32[3,2,4]{2,1,0:T(2,128)}) custom-call(f32[2,8,128]{2,1,0:T(8,128)} %shard_map.50.stat_ref), custom_call_target="tpu_custom_call" | custom-call | tf_op jit(solution)/shard_map/pallas_call | solution.py:556
